TPU v7x, 32 devices: a whole 2x2x4 slice. The times are simulated.
32 devices in a mesh: copy: 4 (over y, x), shard: 2 (over core), model: 4 (over z).
Axes of the slice: x: 2, y: 2, z: 4, core: 2. Of those that a mesh axis runs over, the one named last changes fastest.
Arguments:
- weight_query: bfloat16 [18432, 4096], P(('copy', 'shard'), 'model'), parts along dimension 0, may hold values from -0.125 to 0.125
- low_query: bfloat16 [18432, 32], P(('copy', 'shard')), parts along dimension 0, may hold values from -0.09375 to 0.09375
- high_query: bfloat16 [128, 4096], P('copy', 'model'), parts along dimension 0, may hold values from -1 to 1
- weight_key: bfloat16 [18432, 2048], P(('copy', 'shard'), 'model'), parts along dimension 0, may hold values from -0.125 to 0.125
- low_key: bfloat16 [18432, 32], P(('copy', 'shard')), parts along dimension 0, may hold values from -0.09375 to 0.09375
- high_key: bfloat16 [128, 2048], P('copy', 'model'), parts along dimension 0, may hold values from -1 to 1
- weight_value: bfloat16 [18432, 2048], P(('copy', 'shard'), 'model'), parts along dimension 0, may hold values from -0.125 to 0.125
- low_value: bfloat16 [18432, 32], P(('copy', 'shard')), parts along dimension 0, may hold values from -0.09375 to 0.09375
- high_value: bfloat16 [128, 2048], P('copy', 'model'), parts along dimension 0, may hold values from -1 to 1
- norm_train: float32 [18432], P(('copy', 'shard', 'model')), parts along dimension 0, may hold values from 0.25 to 1.75
- norm_step: float32 [18432], P(('copy', 'shard', 'model')), parts along dimension 0, may hold values from -0.3 to 0.3
Outputs:
- final_query: bfloat16 [18432, 4096], P('copy', 'model'), parts along dimension 0
- final_key: bfloat16 [18432, 2048], P('copy', 'model'), parts along dimension 0
- final_value: bfloat16 [18432, 2048], P('copy', 'model'), parts along dimension 0
- factor_query: float32 [16384], P(('copy', 'model')), parts along dimension 0
- factor_key: float32 [8192], P(('copy', 'model')), parts along dimension 0
- factor_value: float32 [8192], P(('copy', 'model')), parts along dimension 0
- serve_norm: bfloat16 [18432], P('copy'), parts along dimension 0
There are 4 independent parts, one for each index of `copy`. A program takes and returns all parts, laid end to end along the dimension named above; each array names one. Nothing has to cross between parts.
All inputs are finite; a program needn't handle non-finite values. Where the computation divides by a largest or mean magnitude, that divisor is 1e-20 or more.
Results may differ from a plain program's by a relative error of at most 0.001.
Values may be sent and summed in bfloat16 or wider, within the bound.
A program may use at most 128 MiB of HBM per device.

v0:
```python
import jax
import jax.numpy as jnp
from jax import lax
from jax.sharding import PartitionSpec as P

mix_rate = 2.0


def on_device(
    weight_query,
    low_query,
    high_query,
    weight_key,
    low_key,
    high_key,
    weight_value,
    low_value,
    high_value,
    norm_train,
    norm_step,
):
    result_query = weight_query.astype(jnp.float32) + mix_rate * jnp.dot(
        low_query, high_query, preferred_element_type=jnp.float32
    )
    result_key = weight_key.astype(jnp.float32) + mix_rate * jnp.dot(
        low_key, high_key, preferred_element_type=jnp.float32
    )
    result_value = weight_value.astype(jnp.float32) + mix_rate * jnp.dot(
        low_value, high_value, preferred_element_type=jnp.float32
    )
    factor_query, factor_key, factor_value = lax.pmax(
        (
            jnp.max(jnp.abs(result_query), axis=0),
            jnp.max(jnp.abs(result_key), axis=0),
            jnp.max(jnp.abs(result_value), axis=0),
        ),
        "shard",
    )
    narrow_query, narrow_key, narrow_value = (
        (result_query / factor_query).astype(jnp.bfloat16),
        (result_key / factor_key).astype(jnp.bfloat16),
        (result_value / factor_value).astype(jnp.bfloat16),
    )
    final_query, final_key, final_value = (
        lax.all_gather(narrow_query, "shard", axis=0, tiled=True),
        lax.all_gather(narrow_key, "shard", axis=0, tiled=True),
        lax.all_gather(narrow_value, "shard", axis=0, tiled=True),
    )
    serve_norm = lax.all_gather(
        (norm_train + norm_step).astype(jnp.bfloat16), ("shard", "model"), axis=0, tiled=True
    )
    return (final_query, final_key, final_value, factor_query, factor_key, factor_value, serve_norm)


def solution(mesh):
    placed = (
        P(("copy", "shard"), "model"),
        P(("copy", "shard"), None),
        P("copy", "model"),
        P(("copy", "shard"), "model"),
        P(("copy", "shard"), None),
        P("copy", "model"),
        P(("copy", "shard"), "model"),
        P(("copy", "shard"), None),
        P("copy", "model"),
        P(("copy", "shard", "model")),
        P(("copy", "shard", "model")),
    )
    return jax.shard_map(
        on_device,
        mesh=mesh,
        in_specs=placed,
        out_specs=(
            P("copy", "model"),
            P("copy", "model"),
            P("copy", "model"),
            P(("copy", "model")),
            P(("copy", "model")),
            P(("copy", "model")),
            P("copy"),
        ),
        check_vma=False,
    )
```

profile of v0, /device:TPU:0, one launch (start us, length us, event | category | flops | bytes accessed | tf_op | source)
XLA Modules:
  0.0 109.7 jit_solution(4710413063216206264)
XLA Ops:
  7.2 0.0 copy-start
  7.2 0.0 copy-start.7
  7.2 0.0 copy-start.5
  7.2 0.0 copy-start.4
  7.2 0.0 all-gather.6.cloned.1.call-start
  7.3 4.9 %abs_reduce_fusion.2 = (f32[512]{0:T(512)S(1)}, f32[2304,512]{1,0:T(8,128)}) fusion(bf16[2304,32]{0,1:T(8,128)(2,1)} %param.15, bf16[32,512]{1,0:T(8,128)(2,1)} %param.16, bf16[2304,512]{1,0:T(8,128)(2,1)} %param.14), kind=kOutput, calls=%fused_computation.10 | convolution fusion | flops 81395200 | bytes 7260160 | tf_op jit(solution)/shard_map/dot_general | solution.py:25
  12.2 0.0 copy-done.7
  12.2 0.0 copy-done.5
  12.2 0.0 copy-done.4
  12.2 0.0 copy-start.2
  12.2 0.0 copy-start.6
  12.2 3.1 %abs_reduce_fusion.1 = (f32[512]{0:T(512)S(1)}, f32[2304,512]{1,0:T(8,128)}) fusion(bf16[2304,32]{0,1:T(8,128)(2,1)S(1)} %copy-done.5, bf16[32,512]{1,0:T(8,128)(2,1)S(1)} %copy-done.7, bf16[2304,512]{1,0:T(8,128)(2,1)S(1)} %copy-done.4), kind=kOutput, calls=%fused_computation.8 | convolution fusion | flops 81395200 | bytes 7260160 | tf_op jit(solution)/shard_map/dot_general | solution.py:28
  15.3 0.0 copy-done
  15.3 0.7 copy-done.2
  15.9 0.0 copy-done.6
  15.9 5.2 %abs_reduce_fusion = (f32[1024]{0:T(1024)S(1)}, f32[2304,1024]{1,0:T(8,128)}) fusion(bf16[2304,32]{0,1:T(8,128)(2,1)S(1)} %copy-done, bf16[32,1024]{1,0:T(8,128)(2,1)S(1)} %copy-done.6, bf16[2304,1024]{1,0:T(8,128)(2,1)S(1)} %copy-done.2), kind=kOutput, calls=%fused_computation.1 | convolution fusion | flops 162790400 | bytes 14372864 | tf_op jit(solution)/shard_map/dot_general | solution.py:22
  21.1 2.6 %all-reduce.1 = (f32[1024]{0:T(1024)S(1)}, f32[512]{0:T(512)S(1)}, f32[512]{0:T(512)S(1)}) all-reduce(f32[1024]{0:T(1024)S(1)} %get-tuple-element.10, f32[512]{0:T(512)S(1)} %get-tuple-element.12, f32[512]{0:T(512)S(1)} %get-tuple-element.14), channel_id=1, replica_groups=mesh['copy'=4,'shard'=2,'model'=4] {'shard'}, use_global_device_ids=true, to_apply=%region_1.0 | all-reduce | flops 2048 | bytes 16384 | tf_op jit(solution)/shard_map/pmax | solution.py:31
  23.7 0.0 copy-start.11
  23.7 0.0 copy-start.12
  23.7 0.0 copy-start.10
  23.8 4.4 %divide_convert_fusion.2 = bf16[2304,512]{1,0:T(8,128)(2,1)} fusion(f32[2304,512]{1,0:T(8,128)} %get-tuple-element.13, f32[512]{0:T(512)S(1)} %get-tuple-element.27), kind=kLoop, calls=%fused_computation.9 | loop fusion | flops 2359296 | bytes 7079936 | tf_op jit(solution)/shard_map/convert_element_type | solution.py:41
  28.1 0.0 all-gather.6.cloned.1.call-update
  28.2 0.0 copy-done.11
  28.2 0.0 all-gather.8.cloned.1.call-start
  28.2 0.0 copy-done.12
  28.2 4.5 %divide_convert_fusion.1 = bf16[2304,512]{1,0:T(8,128)(2,1)} fusion(f32[2304,512]{1,0:T(8,128)} %get-tuple-element.15, f32[512]{0:T(512)S(1)} %get-tuple-element.28), kind=kLoop, calls=%fused_computation.7 | loop fusion | flops 2359296 | bytes 7079936 | tf_op jit(solution)/shard_map/convert_element_type | solution.py:42
  32.7 0.0 all-gather.8.cloned.1.call-update
  32.7 0.0 all-gather.4.cloned.1.call-start
  32.8 0.0 copy-done.10
  32.8 7.6 %divide_convert_fusion = bf16[2304,1024]{1,0:T(8,128)(2,1)} fusion(f32[2304,1024]{1,0:T(8,128)} %get-tuple-element.11, f32[1024]{0:T(1024)S(1)} %get-tuple-element.26), kind=kLoop, calls=%fused_computation | loop fusion | flops 4718592 | bytes 14159872 | tf_op jit(solution)/shard_map/convert_element_type | solution.py:40
  40.3 0.0 copy-start.13
  40.3 0.0 copy-start.8
  40.3 0.0 copy-start.9
  40.3 0.0 all-gather.4.cloned.1.call-update
  40.4 0.6 copy-done.13
  41.0 0.6 dynamic-slice
  42.2 0.0 copy-done.8
  42.3 0.0 copy-done.9
  42.3 0.2 dynamic-update-slice
  42.5 30.9 %all-reduce = bf16[4608]{0:T(1024)(128)(2,1)} all-reduce(bf16[4608]{0:T(1024)(128)(2,1)S(1)} %dynamic-update-slice), channel_id=1, replica_groups=mesh['copy'=4,'shard'=2,'model'=4] {'shard','model'}, use_global_device_ids=true, to_apply=%add | all-reduce | flops 4608 | bytes 18432
  73.4 0.0 all-gather.6.cloned.1.call-done
  73.4 0.0 all-gather.8.cloned.1.call-done
  73.4 14.1 %all-gather.4.cloned.1.call-done = bf16[4608,1024]{1,0:T(8,128)(2,1)} async-done(((bf16[2304,1024]{1,0:T(8,128)(2,1)}), bf16[4608,1024]{1,0:T(8,128)(2,1)}) %all-gather.4.cloned.1.call-update) | async-done | bytes 9437200 | tf_op jit(solution)/shard_map/all_gather | solution.py:45
  87.5 8.5 %copy.22 = bf16[4608,1024]{1,0:T(8,128)(2,1)} copy(bf16[4608,1024]{1,0:T(8,128)(2,1)} %all-gather.4.cloned.1.call-done) | data formatting | bytes 18874368
  96.0 0.0 copy-start.3
  96.0 0.0 copy-start.1
  96.0 5.0 %copy.23 = bf16[4608,512]{1,0:T(8,128)(2,1)} copy(bf16[4608,512]{1,0:T(8,128)(2,1)} %all-gather.6.cloned.1.call-done) | data formatting | bytes 9437184
  101.0 0.0 copy-done.3
  101.0 2.2 %copy.24 = bf16[4608,512]{1,0:T(8,128)(2,1)} copy(bf16[4608,512]{1,0:T(8,128)(2,1)S(1)} %copy-done.3) | data formatting | bytes 9437184
  103.2 0.0 copy-done.1
  (2 shorter events, 0.0 us)
Async XLA Ops:
  7.2 8.1 %copy-start = (bf16[2304,32]{0,1:T(8,128)(2,1)S(1)}, bf16[2304,32]{0,1:T(8,128)(2,1)}, u32[]{:S(2)}) copy-start(bf16[2304,32]{0,1:T(8,128)(2,1)} %param.12) | copy-start | bytes 442372
  7.2 5.0 %copy-start.7 = (bf16[32,512]{1,0:T(8,128)(2,1)S(1)}, bf16[32,512]{1,0:T(8,128)(2,1)}, u32[]{:S(2)}) copy-start(bf16[32,512]{1,0:T(8,128)(2,1)} %param.19) | copy-start | bytes 98308
  7.2 5.0 %copy-start.5 = (bf16[2304,32]{0,1:T(8,128)(2,1)S(1)}, bf16[2304,32]{0,1:T(8,128)(2,1)}, u32[]{:S(2)}) copy-start(bf16[2304,32]{0,1:T(8,128)(2,1)} %param.18) | copy-start | bytes 442372
  7.2 5.0 %copy-start.4 = (bf16[2304,512]{1,0:T(8,128)(2,1)S(1)}, bf16[2304,512]{1,0:T(8,128)(2,1)}, u32[]{:S(2)}) copy-start(bf16[2304,512]{1,0:T(8,128)(2,1)} %param.17) | copy-start | bytes 7077892
  7.2 66.2 %all-gather.6.cloned.1.call-start = ((), (), s32[]{:S(2)}) async-start(), calls=%async_computation.1 | async-start | bytes 7077888 | tf_op jit(solution)/shard_map/all_gather | solution.py:46
  12.2 3.8 %copy-start.2 = (bf16[2304,1024]{1,0:T(8,128)(2,1)S(1)}, bf16[2304,1024]{1,0:T(8,128)(2,1)}, u32[]{:S(2)}) copy-start(bf16[2304,1024]{1,0:T(8,128)(2,1)} %param.11) | copy-start | bytes 14155780
  12.2 3.8 %copy-start.6 = (bf16[32,1024]{1,0:T(8,128)(2,1)S(1)}, bf16[32,1024]{1,0:T(8,128)(2,1)}, u32[]{:S(2)}) copy-start(bf16[32,1024]{1,0:T(8,128)(2,1)} %param.13) | copy-start | bytes 196612
  23.7 4.4 %copy-start.11 = (f32[512]{0:T(512)}, f32[512]{0:T(512)S(1)}, u32[]{:S(2)}) copy-start(f32[512]{0:T(512)S(1)} %get-tuple-element.27) | copy-start | bytes 6148
  23.7 4.5 %copy-start.12 = (f32[512]{0:T(512)}, f32[512]{0:T(512)S(1)}, u32[]{:S(2)}) copy-start(f32[512]{0:T(512)S(1)} %get-tuple-element.28) | copy-start | bytes 6148
  23.7 9.0 %copy-start.10 = (f32[1024]{0:T(1024)}, f32[1024]{0:T(1024)S(1)}, u32[]{:S(2)}) copy-start(f32[1024]{0:T(1024)S(1)} %get-tuple-element.26) | copy-start | bytes 12292
  28.2 45.3 %all-gather.8.cloned.1.call-start = ((), (), s32[]{:S(2)}) async-start(), calls=%async_computation.2 | async-start | bytes 7077888 | tf_op jit(solution)/shard_map/all_gather | solution.py:47
  32.7 54.8 %all-gather.4.cloned.1.call-start = ((), (), s32[]{:S(2)}) async-start(), calls=%async_computation | async-start | bytes 14155776 | tf_op jit(solution)/shard_map/all_gather | solution.py:45
  40.3 0.7 copy-start.13
  40.3 1.9 %copy-start.8 = (f32[576]{0:T(1024)S(1)}, f32[576]{0:T(1024)}, u32[]{:S(2)}) copy-start(f32[576]{0:T(1024)} %param.20) | copy-start | bytes 6916
  40.3 1.9 %copy-start.9 = (f32[576]{0:T(1024)S(1)}, f32[576]{0:T(1024)}, u32[]{:S(2)}) copy-start(f32[576]{0:T(1024)} %param.21) | copy-start | bytes 6916
  96.0 5.0 %copy-start.3 = (bf16[4608,512]{1,0:T(8,128)(2,1)S(1)}, bf16[4608,512]{1,0:T(8,128)(2,1)}, u32[]{:S(2)}) copy-start(bf16[4608,512]{1,0:T(8,128)(2,1)} %all-gather.8.cloned.1.call-done) | copy-start | bytes 14155780
  96.0 7.2 %copy-start.1 = (bf16[2304,32]{0,1:T(8,128)(2,1)S(1)}, bf16[2304,32]{0,1:T(8,128)(2,1)}, u32[]{:S(2)}) copy-start(bf16[2304,32]{0,1:T(8,128)(2,1)} %param.12) | copy-start | bytes 442372
Sparse Core Ops, SparseCore 0:
  28.3 16.9 all-gather.5
  46.9 15.5 all-gather.7
  64.6 22.7 all-gather.3
where the time goes:
time: 110 us
  blocking collectives  33.5 us (30%)
  local copies, waits for them, and re-layouts  17.9 us (16%)
  other arithmetic  16.4 us (15%)
  between operations  14.5 us (13%)
  waiting for transfers between devices  14.1 us (13%)
  matrix products  13.2 us (12%)
    unnamed x1, blocking collectives  30.9 us
    unnamed x34, local copies, waits for them, and re-layouts  17.9 us
    all_gather x1, waiting for transfers between devices, on_device(): lax.all_gather(narrow_query, 'shard', axis=0, tiled=True)  14.1 us
    convert_element_type x1, other arithmetic, on_device(): (result_query / factor_query).astype(jnp.bfloat16)  7.58 us
    dot_general x1, matrix products, on_device(): jnp.dot(low_query, high_query, preferred_element_type=jnp.float32)  5.16 us
    dot_general x1, matrix products, on_device(): jnp.dot(low_key, high_key, preferred_element_type=jnp.float32)  4.89 us
    convert_element_type x1, other arithmetic, on_device(): (result_value / factor_value).astype(jnp.bfloat16)  4.45 us
    convert_element_type x1, other arithmetic, on_device(): (result_key / factor_key).astype(jnp.bfloat16)  4.38 us
  transfers between devices with their start and end apart: 3, of which 1 were waited for; matrix products, arithmetic and copies ran while one was open for 12% of the time, Pallas kernels for 0%

commit v1 on v0

v1 whole, which is shorter than its diff:
```python
import functools

import jax
import jax.numpy as jnp
from jax import lax
from jax.experimental import pallas as pl
from jax.experimental.pallas import tpu as pltpu
from jax.sharding import PartitionSpec as P

mix_rate = 2.0
MESH = pl.DeviceIdType.MESH


def chunk_of(rows):
    return max(c for c in range(16, 257, 16) if rows % c == 0)


def merge_kernel(n, *refs):
    parts, lows = refs[:n], refs[n : 2 * n]
    high_ref, out_ref, factor_ref, held = refs[2 * n :]
    me = lax.axis_index("shard")
    rows, columns = parts[0].shape
    chunk = chunk_of(rows)
    high = high_ref[...]
    top = jnp.zeros((8, columns), jnp.float32)
    for k in range(n):

        def first(i, top, k=k):
            at = pl.ds(pl.multiple_of(i * chunk, chunk), chunk)
            result = parts[k][at, :].astype(jnp.float32) + jnp.dot(
                lows[k][at, :], high, preferred_element_type=jnp.float32
            )
            held[pl.ds(pl.multiple_of(k * rows + i * chunk, 16), chunk), :] = result
            return jnp.maximum(top, jnp.max(jnp.abs(result).reshape(chunk // 8, 8, columns), axis=0))

        top = lax.fori_loop(0, rows // chunk, first, top)
    factor = jnp.max(top, axis=0, keepdims=True)
    factor_ref[...] = factor
    scale = 1.0 / factor
    for k in range(n):
        base = lax.rem(me + k, n) * rows

        def second(i, carry, k=k, base=base):
            value = held[pl.ds(pl.multiple_of(k * rows + i * chunk, 16), chunk), :] * scale
            out_ref[pl.ds(pl.multiple_of(base + i * chunk, 16), chunk), :] = value.astype(out_ref.dtype)
            return carry

        lax.fori_loop(0, rows // chunk, second, 0)


def merge(n, parts, lows, high):
    rows, columns = parts[0].shape
    width = 256 if columns % 256 == 0 else 128
    depth = high.shape[0]
    final, factor = pl.pallas_call(
        functools.partial(merge_kernel, n),
        grid=(columns // width,),
        out_shape=(
            jax.ShapeDtypeStruct((n * rows, columns), jnp.bfloat16),
            jax.ShapeDtypeStruct((1, columns), jnp.float32),
        ),
        in_specs=[pl.BlockSpec((rows, width), lambda j: (0, j))] * n
        + [pl.BlockSpec((rows, depth), lambda j: (0, 0))] * n
        + [pl.BlockSpec((depth, width), lambda j: (0, j))],
        out_specs=(
            pl.BlockSpec((n * rows, width), lambda j: (0, j)),
            pl.BlockSpec((1, width), lambda j: (0, j)),
        ),
        scratch_shapes=[pltpu.VMEM((n * rows, width), jnp.float32)],
        compiler_params=pltpu.CompilerParams(vmem_limit_bytes=24 * 2**20),
        cost_estimate=pl.CostEstimate(
            flops=2 * n * rows * columns * depth, bytes_accessed=4 * n * rows * columns, transcendentals=0
        ),
    )(*parts, *lows, high)
    return final, factor.reshape(columns)


def norm_kernel(shards, models, own_ref, all_ref, send_sem, recv_sem):
    shard, model = lax.axis_index("shard"), lax.axis_index("model")
    me = shard * models + model
    others = [
        (lax.rem(shard + s, shards), lax.rem(model + m, models), s * models + m)
        for s in range(shards)
        for m in range(models)
        if s or m
    ]
    barrier = pltpu.get_barrier_semaphore()
    for s, m, _ in others:
        pl.semaphore_signal(barrier, inc=1, device_id={"shard": s, "model": m}, device_id_type=MESH)
    pl.semaphore_wait(barrier, len(others))
    copies = []
    for s, m, k in others:
        copy = pltpu.make_async_remote_copy(
            src_ref=own_ref,
            dst_ref=all_ref.at[me],
            send_sem=send_sem.at[k],
            recv_sem=recv_sem.at[k],
            device_id={"shard": s, "model": m},
            device_id_type=MESH,
        )
        copy.start()
        copies.append(copy)
    all_ref[me] = own_ref[...]
    for copy in copies:
        copy.wait()


def gather_norm(shards, models, own):
    count = shards * models
    size = own.shape[0]
    return pl.pallas_call(
        functools.partial(norm_kernel, shards, models),
        out_shape=jax.ShapeDtypeStruct((count, 1, size), own.dtype),
        in_specs=[pl.BlockSpec(memory_space=pltpu.VMEM)],
        out_specs=pl.BlockSpec(memory_space=pltpu.VMEM),
        scratch_shapes=[pltpu.SemaphoreType.DMA((count,)), pltpu.SemaphoreType.DMA((count,))],
        compiler_params=pltpu.CompilerParams(collective_id=0, has_side_effects=True, vmem_limit_bytes=2**20),
    )(own.reshape(1, size)).reshape(count * size)


def on_device(
    shards,
    models,
    weight_query,
    low_query,
    high_query,
    weight_key,
    low_key,
    high_key,
    weight_value,
    low_value,
    high_value,
    norm_train,
    norm_step,
):
    def spread(array):
        return [array] + [
            lax.ppermute(array, "shard", [((d + k) % shards, d) for d in range(shards)]) for k in range(1, shards)
        ]

    rank = low_query.shape[1]
    depth = -(-3 * rank // 128) * 128
    low = jnp.concatenate([low_query, low_key, low_value], axis=1)
    low = jnp.pad(low, ((0, 0), (0, depth - 3 * rank)))
    highs = [
        jnp.pad(mix_rate * high, ((k * rank, depth - (k + 1) * rank), (0, 0)))
        for k, high in enumerate((high_query, high_key, high_value))
    ]
    lows = spread(low)
    serve_norm = gather_norm(shards, models, (norm_train + norm_step).astype(jnp.bfloat16))
    final_query, factor_query = merge(shards, spread(weight_query), lows, highs[0])
    final_key, factor_key = merge(shards, spread(weight_key), lows, highs[1])
    final_value, factor_value = merge(shards, spread(weight_value), lows, highs[2])
    return (final_query, final_key, final_value, factor_query, factor_key, factor_value, serve_norm)


def solution(mesh):
    placed = (
        P(("copy", "shard"), "model"),
        P(("copy", "shard"), None),
        P("copy", "model"),
        P(("copy", "shard"), "model"),
        P(("copy", "shard"), None),
        P("copy", "model"),
        P(("copy", "shard"), "model"),
        P(("copy", "shard"), None),
        P("copy", "model"),
        P(("copy", "shard", "model")),
        P(("copy", "shard", "model")),
    )
    return jax.shard_map(
        functools.partial(on_device, mesh.shape["shard"], mesh.shape["model"]),
        mesh=mesh,
        in_specs=placed,
        out_specs=(
            P("copy", "model"),
            P("copy", "model"),
            P("copy", "model"),
            P(("copy", "model")),
            P(("copy", "model")),
            P(("copy", "model")),
            P("copy"),
        ),
        check_vma=False,
    )
```

time: 110 us -> 63.1 us (0.57)
  Pallas kernels: 0 us -> 45.1 us
  blocking collectives: 33.5 us -> 0 us
  waiting for transfers between devices: 14.1 us -> 0.01 us
  between operations: 14.5 us -> 0.75 us
  matrix products: 13.2 us -> 0 us
  other arithmetic: 16.4 us -> 3.49 us
  local copies, waits for them, and re-layouts: 17.9 us -> 12.1 us
    pallas_call x0 -> x4, Pallas kernels: none -> 45.1 us  [the longest x3 37.8 us: merge(): pl.pallas_call(functools.partial(merge_kernel, n), grid=(columns // width...]
    unnamed x1 -> x0, blocking collectives: 30.9 us -> none
    convert_element_type x3 -> x0, other arithmetic: 16.4 us -> none  [the longest x1 7.58 us: on_device(): (result_query / factor_query).astype(jnp.bfloat16)]
    all_gather x3 -> x0, waiting for transfers between devices: 14.1 us -> none  [the longest x1 14.1 us: on_device(): lax.all_gather(narrow_query, 'shard', axis=0, tiled=True)]
    dot_general x3 -> x0, matrix products: 13.2 us -> none  [the longest x1 5.16 us: on_device(): jnp.dot(low_query, high_query, preferred_element_type=jnp.float32)]
    unnamed x34 -> x25, local copies, waits for them, and re-layouts: 17.9 us -> 9.33 us
    pmax x1 -> x0, blocking collectives: 2.62 us -> none  [on_device(): lax.pmax((jnp.max(jnp.abs(result_query), axis=0), jnp.max(jnp.abs(result_...]
    pad x0 -> x3, local copies, waits for them, and re-layouts: none -> 2.05 us  [on_device(): jnp.pad(mix_rate * high, ((k * rank, depth - (k + 1) * rank), (0, 0)))]
  transfers between devices with their start and end apart: 3 -> 4, of which waited for: 1 -> 0; matrix products, arithmetic and copies ran while one was open for 12% -> 18% of each run, Pallas kernels for 0% -> 44%
where the time goes in v1:
time: 63.1 us; the launch traced here: 62.7 us
  Pallas kernels  45.1 us (71%)
  local copies, waits for them, and re-layouts  12.1 us (19%)
  other arithmetic  3.49 us (6%)
  starting transfers between devices  1.21 us (2%)
  between operations  0.75 us (1%)
    pallas_call x3, Pallas kernels, merge(): pl.pallas_call(functools.partial(merge_kernel, n), grid=(columns // width...  37.8 us
    unnamed x25, local copies, waits for them, and re-layouts  9.33 us
    pallas_call x1, Pallas kernels, gather_norm(): pl.pallas_call(functools.partial(norm_kernel, shards, models), out_shape=...  7.38 us
    pad x3, local copies, waits for them, and re-layouts, on_device(): jnp.pad(mix_rate * high, ((k * rank, depth - (k + 1) * rank), (0, 0)))  2.05 us
    concatenate x1, other arithmetic, on_device(): low = jnp.concatenate([low_query, low_key, low_value], axis=1)  1.92 us
  transfers between devices with their start and end apart: 4, of which 0 were waited for; matrix products, arithmetic and copies ran while one was open for 18% of the time, Pallas kernels for 44%

profile of v1, /device:TPU:0, one launch (start us, length us, event | category | flops | bytes accessed | tf_op | source)
XLA Modules:
  0.0 62.7 jit_solution(11083291613189061231)
XLA Ops:
  0.6 0.6 collective-permute-start
  1.2 0.1 collective-permute-start.2
  1.3 0.4 collective-permute-start.3
  1.7 1.2 %copy.21 = bf16[2304,32]{1,0:T(8,128)(2,1)S(1)} copy(bf16[2304,32]{0,1:T(8,128)(2,1)} %param.12) | data formatting | bytes 294912 | tf_op args[1]
  2.9 0.0 copy-start.9
  2.9 0.0 copy-start.10
  3.0 0.0 copy-start.1
  3.0 2.1 %copy.22 = bf16[2304,32]{1,0:T(8,128)(2,1)} copy(bf16[2304,32]{0,1:T(8,128)(2,1)} %param.15) | data formatting | bytes 294912 | tf_op args[4]
  5.1 2.0 %copy.23 = bf16[2304,32]{1,0:T(8,128)(2,1)} copy(bf16[2304,32]{0,1:T(8,128)(2,1)} %param.18) | data formatting | bytes 294912 | tf_op args[7]
  7.1 0.0 copy-start.7
  7.1 0.0 copy-start.8
  7.1 1.9 %fusion.4.refs_2_ = bf16[2304,128]{1,0:T(8,128)(2,1)S(1)} fusion(bf16[2304,32]{1,0:T(8,128)(2,1)} %copy.23, bf16[2304,32]{1,0:T(8,128)(2,1)} %copy.22, bf16[2304,32]{1,0:T(8,128)(2,1)S(1)} %copy.21), kind=kLoop, calls=%fused_computation.5 | loop fusion | flops 2949120 | bytes 1032192 | tf_op jit(solution)/shard_map/concatenate | solution.py:143
  9.0 0.1 collective-permute-start.1
  9.1 0.0 copy-done.7
  9.1 0.7 %pad.17.refs_4_ = bf16[128,1024]{1,0:T(8,128)(2,1)} pad(bf16[32,1024]{1,0:T(8,128)(2,1)S(1)} %broadcast_multiply_fusion, bf16[]{:T(256)} %constant.2.clone.1), padding=0_96x0_0 | pad | bytes 327682 | tf_op jit(solution)/shard_map/jit(_pad)/pad | solution.py:146
  9.9 0.0 copy-done.8
  9.9 0.7 %pad.18.refs_4_ = bf16[128,512]{1,0:T(8,128)(2,1)} pad(bf16[32,512]{1,0:T(8,128)(2,1)S(1)} %broadcast_multiply_fusion.2, bf16[]{:T(256)} %constant.2.clone.1), padding=32_64x0_0 | pad | bytes 163842 | tf_op jit(solution)/shard_map/jit(_pad)/pad | solution.py:146
  10.5 0.8 %broadcast_multiply_fusion.1 = bf16[32,512]{1,0:T(8,128)(2,1)S(1)} fusion(bf16[32,512]{1,0:T(8,128)(2,1)} %param.19), kind=kLoop, calls=%fused_computation.7 | loop fusion | flops 16384 | bytes 65536 | tf_op jit(solution)/shard_map/mul | solution.py:146
  11.3 0.7 %pad.19.refs_4_ = bf16[128,512]{1,0:T(8,128)(2,1)} pad(bf16[32,512]{1,0:T(8,128)(2,1)S(1)} %broadcast_multiply_fusion.1, bf16[]{:T(256)} %constant.2.clone.1), padding=64_32x0_0 | pad | bytes 163842 | tf_op jit(solution)/shard_map/jit(_pad)/pad | solution.py:146
  12.0 0.0 copy-done.9
  12.0 0.0 copy-done.10
  12.0 7.4 %shard_map.165 = bf16[8,1,576]{2,1,0:T(2,128)(2,1)S(1)} custom-call(bf16[1,576]{1,0:T(2,128)(2,1)S(1)} %reshape.32.own_ref), custom_call_target="tpu_custom_call" | custom-call | tf_op jit(solution)/shard_map/pallas_call | solution.py:111
  19.4 0.0 copy-start.6
  19.4 0.6 copy-done.6
  20.0 0.8 %reduce = bf16[8,576]{1,0:T(8,128)(2,1)S(1)} reduce(bf16[8,1,576]{2,1,0:T(2,128)(2,1)} %copy-done.6, bf16[]{:T(256)} %constant.14), dimensions={1}, to_apply=%pallas_call.27.reduce_sub_computation | reduce | bytes 18434 | tf_op jit(solution)/shard_map/pallas_call | solution.py:111
  20.8 0.7 %reshape.33 = bf16[4608]{0:T(1024)(128)(2,1)} reshape(bf16[8,576]{1,0:T(8,128)(2,1)S(1)} %reduce) | data formatting | bytes 18432 | tf_op jit(solution)/shard_map/reshape | solution.py:118
  21.5 0.0 copy-start.2
  21.5 0.0 copy-start.4
  21.5 0.0 collective-permute-done.1.refs_3_
  21.5 0.0 collective-permute-done.2.refs_1_
  21.5 0.0 copy-done.1
  21.5 0.0 copy-start.5
  21.5 1.0 %copy-done.5 = bf16[128,512]{1,0:T(8,128)(2,1)S(1)} copy-done((bf16[128,512]{1,0:T(8,128)(2,1)S(1)}, bf16[128,512]{1,0:T(8,128)(2,1)}, u32[]{:S(2)}) %copy-start.5) | copy-done | bytes 131096
  22.6 10.0 %shard_map.163 = (bf16[4608,512]{1,0:T(8,128)(2,1)}, f32[1,512]{1,0:T(1,128)}) custom-call(bf16[2304,512]{1,0:T(8,128)(2,1)S(1)} %copy-done.1, bf16[2304,512]{1,0:T(8,128)(2,1)} %collective-permute-done.2.refs_1_, bf16[2304,128]{1,0:T(8,128)(2,1)S(1)} %fusion.4.refs_2_, bf16[2304,128]{1,0:T(8,128)(2,1)S(1)} %collective-permute-done.1.refs_3_, ...), custom_call_target="tpu_custom_call" | custom-call | flops 603979776 | bytes 9437184 | tf_op jit(solution)/shard_map/pallas_call | solution.py:55
  32.6 0.0 copy-start.3
  32.6 0.0 collective-permute-done.3.refs_1_
  32.6 0.0 copy-done.2
  32.6 0.0 copy-done.4
  32.6 10.0 %shard_map.164 = (bf16[4608,512]{1,0:T(8,128)(2,1)}, f32[1,512]{1,0:T(1,128)}) custom-call(bf16[2304,512]{1,0:T(8,128)(2,1)S(1)} %copy-done.2, bf16[2304,512]{1,0:T(8,128)(2,1)} %collective-permute-done.3.refs_1_, bf16[2304,128]{1,0:T(8,128)(2,1)S(1)} %fusion.4.refs_2_, bf16[2304,128]{1,0:T(8,128)(2,1)S(1)} %collective-permute-done.1.refs_3_, ...), custom_call_target="tpu_custom_call" | custom-call | flops 603979776 | bytes 9437184 | tf_op jit(solution)/shard_map/pallas_call | solution.py:55
  42.6 0.0 collective-permute-done.refs_1_
  42.6 0.0 copy-done.3
  42.6 0.0 copy-start
  42.6 2.3 %copy-done = bf16[2304,1024]{1,0:T(8,128)(2,1)S(1)} copy-done((bf16[2304,1024]{1,0:T(8,128)(2,1)S(1)}, bf16[2304,1024]{1,0:T(8,128)(2,1)}, u32[]{:S(2)}) %copy-start) | copy-done | bytes 4718616
  45.0 17.7 %shard_map.162 = (bf16[4608,1024]{1,0:T(8,128)(2,1)}, f32[1,1024]{1,0:T(1,128)}) custom-call(bf16[2304,1024]{1,0:T(8,128)(2,1)S(1)} %copy-done, bf16[2304,1024]{1,0:T(8,128)(2,1)} %collective-permute-done.refs_1_, bf16[2304,128]{1,0:T(8,128)(2,1)S(1)} %fusion.4.refs_2_, bf16[2304,128]{1,0:T(8,128)(2,1)S(1)} %collective-permute-done.1.refs_3_, ...), custom_call_target="tpu_custom_call" | custom-call | flops 1207959552 | bytes 18874368 | tf_op jit(solution)/shard_map/pallas_call | solution.py:55
  (4 shorter events, 0.0 us)
Async XLA Ops:
  0.6 42.0 %collective-permute-start = (bf16[2304,1024]{1,0:T(8,128)(2,1)}, bf16[2304,1024]{1,0:T(8,128)(2,1)}, u32[]{:S(2)}, u32[]{:S(2)}) collective-permute-start(bf16[2304,1024]{1,0:T(8,128)(2,1)} %refs_0_.3), channel_id=1, source_target_pairs={{4,0},{0,4},{5,1},{1,5},{6,2},{2,6},{7,3},{3,7},{12,8},{8,12},{13,... | collective-permute-start | bytes 14155784 | tf_op jit(solution)/shard_map/ppermute | solution.py:138
  1.2 20.3 %collective-permute-start.2 = (bf16[2304,512]{1,0:T(8,128)(2,1)}, bf16[2304,512]{1,0:T(8,128)(2,1)}, u32[]{:S(2)}, u32[]{:S(2)}) collective-permute-start(bf16[2304,512]{1,0:T(8,128)(2,1)} %refs_0_.4), channel_id=1, source_target_pairs={{4,0},{0,4},{5,1},{1,5},{6,2},{2,6},{7,3},{3,7},{12,8},{8,12},{13,... | collective-permute-start | bytes 7077896 | tf_op jit(solution)/shard_map/ppermute | solution.py:138
  1.3 31.3 %collective-permute-start.3 = (bf16[2304,512]{1,0:T(8,128)(2,1)}, bf16[2304,512]{1,0:T(8,128)(2,1)}, u32[]{:S(2)}, u32[]{:S(2)}) collective-permute-start(bf16[2304,512]{1,0:T(8,128)(2,1)} %refs_0_.5), channel_id=1, source_target_pairs={{4,0},{0,4},{5,1},{1,5},{6,2},{2,6},{7,3},{3,7},{12,8},{8,12},{13,... | collective-permute-start | bytes 7077896 | tf_op jit(solution)/shard_map/ppermute | solution.py:138
  2.9 9.0 %copy-start.9 = (f32[576]{0:T(1024)S(1)}, f32[576]{0:T(1024)}, u32[]{:S(2)}) copy-start(f32[576]{0:T(1024)} %param.20) | copy-start | bytes 6916
  2.9 9.0 %copy-start.10 = (f32[576]{0:T(1024)S(1)}, f32[576]{0:T(1024)}, u32[]{:S(2)}) copy-start(f32[576]{0:T(1024)} %param.21) | copy-start | bytes 6916
  3.0 18.5 %copy-start.1 = (bf16[2304,512]{1,0:T(8,128)(2,1)S(1)}, bf16[2304,512]{1,0:T(8,128)(2,1)}, u32[]{:S(2)}) copy-start(bf16[2304,512]{1,0:T(8,128)(2,1)} %refs_0_.4) | copy-start | bytes 7077892
  7.1 2.1 %copy-start.7 = (bf16[32,1024]{1,0:T(8,128)(2,1)S(1)}, bf16[32,1024]{1,0:T(8,128)(2,1)}, u32[]{:S(2)}) copy-start(bf16[32,1024]{1,0:T(8,128)(2,1)} %param.13) | copy-start | bytes 196612
  7.1 2.8 %copy-start.8 = (bf16[32,512]{1,0:T(8,128)(2,1)S(1)}, bf16[32,512]{1,0:T(8,128)(2,1)}, u32[]{:S(2)}) copy-start(bf16[32,512]{1,0:T(8,128)(2,1)} %param.16) | copy-start | bytes 98308
  9.0 12.5 %collective-permute-start.1 = (bf16[2304,128]{1,0:T(8,128)(2,1)S(1)}, bf16[2304,128]{1,0:T(8,128)(2,1)S(1)}, u32[]{:S(2)}, u32[]{:S(2)}) collective-permute-start(bf16[2304,128]{1,0:T(8,128)(2,1)S(1)} %fusion.4.refs_2_), channel_id=1, source_target_pairs={{4,0},{0,4},{5,1},{1,5},{6,2},{2,6},{7,3},{3,7},{12,8},{8,12},{13,... | collective-permute-start | bytes 1769480 | tf_op jit(solution)/shard_map/ppermute | solution.py:138
  19.4 0.6 copy-start.6
  21.5 11.1 %copy-start.2 = (bf16[2304,512]{1,0:T(8,128)(2,1)S(1)}, bf16[2304,512]{1,0:T(8,128)(2,1)}, u32[]{:S(2)}) copy-start(bf16[2304,512]{1,0:T(8,128)(2,1)} %refs_0_.5) | copy-start | bytes 7077892
  21.5 11.1 %copy-start.4 = (bf16[128,512]{1,0:T(8,128)(2,1)S(1)}, bf16[128,512]{1,0:T(8,128)(2,1)}, u32[]{:S(2)}) copy-start(bf16[128,512]{1,0:T(8,128)(2,1)} %pad.19.refs_4_) | copy-start | bytes 393220
  21.5 1.1 %copy-start.5 = (bf16[128,512]{1,0:T(8,128)(2,1)S(1)}, bf16[128,512]{1,0:T(8,128)(2,1)}, u32[]{:S(2)}) copy-start(bf16[128,512]{1,0:T(8,128)(2,1)} %pad.18.refs_4_) | copy-start | bytes 393220
  32.6 10.1 %copy-start.3 = (bf16[128,1024]{1,0:T(8,128)(2,1)S(1)}, bf16[128,1024]{1,0:T(8,128)(2,1)}, u32[]{:S(2)}) copy-start(bf16[128,1024]{1,0:T(8,128)(2,1)} %pad.17.refs_4_) | copy-start | bytes 786436
  42.6 2.3 %copy-start = (bf16[2304,1024]{1,0:T(8,128)(2,1)S(1)}, bf16[2304,1024]{1,0:T(8,128)(2,1)}, u32[]{:S(2)}) copy-start(bf16[2304,1024]{1,0:T(8,128)(2,1)} %refs_0_.3) | copy-start | bytes 14155780
